TPU v7x, 64 devices: a 2x2x8 block of a 4x4x8 slice. The times are simulated.
64 devices in a mesh: req: 4 (over x, y), cp: 16 (over z, core).
Axes of the slice: x: 2, y: 2, z: 8, core: 2. Of those that a mesh axis runs over, the one named last changes fastest.
The devices are a block of a 4x4x8 slice.
Arguments:
- hidden: bfloat16 [4096, 2048], P(('req', 'cp')), parts along dimension 0
- positions: int32 [4096], P(('req', 'cp')), parts along dimension 0
- gain_attn: bfloat16 [3, 2048], replicated
- gain_mlp: bfloat16 [3, 2048], replicated
- w_query: bfloat16 [3, 2048, 16, 128], replicated
- w_key: bfloat16 [3, 2048, 16, 128], replicated
- w_value: bfloat16 [3, 2048, 16, 128], replicated
- w_out: bfloat16 [3, 16, 128, 2048], replicated
- w_gate: bfloat16 [3, 2048, 5504], replicated
- w_up: bfloat16 [3, 2048, 5504], replicated
- w_down: bfloat16 [3, 5504, 2048], replicated
Outputs:
- output 1: bfloat16 [4096, 2048], P(('req', 'cp')), parts along dimension 0
- output 2: bfloat16 [3, 4096, 16, 128], P(None, 'req', 'cp'), parts along dimension 1
- output 3: bfloat16 [3, 4096, 16, 128], P(None, 'req', 'cp'), parts along dimension 1
There are 4 independent parts. A program takes and returns all parts, laid end to end along the dimension named above; an argument that names none is the same for every part.
All inputs are finite; a program needn't handle non-finite values.
Results may differ from a plain program's by a relative error of at most 0.02.
Values are sent between devices in bfloat16 or wider.
A program may use at most 768 MiB of HBM per device.

v0:
```python
import jax
import jax.numpy as jnp
from jax import lax
from jax.sharding import PartitionSpec as P

NORM_EPS = 1e-5
ROPE_BASE = 10000.0


def rms_norm(values, gain_vec):
    wide_vals = values.astype(jnp.float32)
    inv_rms = lax.rsqrt(jnp.mean(wide_vals * wide_vals, axis=-1, keepdims=True) + NORM_EPS)
    return (wide_vals * inv_rms * gain_vec.astype(jnp.float32)).astype(jnp.bfloat16)


def rope_tables(pos_vec, head_dim):
    inv_freq = ROPE_BASE ** (-jnp.arange(0, head_dim, 2, dtype=jnp.float32) / head_dim)
    angles = pos_vec.astype(jnp.float32)[..., None] * inv_freq
    return jnp.cos(angles)[..., None, :], jnp.sin(angles)[..., None, :]


def rotate_half(values, cos_tab, sin_tab):
    half_dim = values.shape[-1] // 2
    lower_half = values[..., :half_dim]
    upper_half = values[..., half_dim:]
    return jnp.concatenate([lower_half * cos_tab - upper_half * sin_tab, upper_half * cos_tab + lower_half * sin_tab], axis=-1)


def to_natural(rows, cp_size):
    lead_dim = rows.shape[0]
    seq_len = rows.shape[1]
    split_rows = rows.reshape((lead_dim, cp_size, 2, seq_len // (2 * cp_size)) + rows.shape[2:])
    natural = jnp.concatenate([split_rows[:, :, 0], split_rows[:, ::-1, 1]], axis=1)
    return natural.reshape(rows.shape)


def attend(queries, key_all, value_all, pos_local, pos_all):
    num_tok = queries.shape[0]
    num_heads = queries.shape[1]
    head_dim = queries.shape[2]
    kv_heads = key_all.shape[1]
    grouped = queries.reshape(num_tok, kv_heads, num_heads // kv_heads, head_dim)
    scores = jnp.einsum("tkgd,skd->kgts", grouped, key_all, preferred_element_type=jnp.float32) * (head_dim ** -0.5)
    allowed = pos_all[None, :] <= pos_local[:, None]
    scores = jnp.where(allowed, scores, -jnp.inf)
    row_max = jnp.max(scores, axis=-1, keepdims=True)
    exp_scores = jnp.exp(scores - row_max)
    attn_probs = (exp_scores / jnp.sum(exp_scores, axis=-1, keepdims=True)).astype(jnp.bfloat16)
    attn_out = jnp.einsum("kgts,skd->tkgd", attn_probs, value_all, preferred_element_type=jnp.float32)
    return attn_out.astype(jnp.bfloat16).reshape(num_tok, num_heads, head_dim)


def solution(mesh):
    cp_size = mesh.shape["cp"]
    row_spec = P(("req", "cp"), None)
    pos_spec = P(("req", "cp"))
    rep_spec = P()
    cache_spec = P(None, "req", "cp", None)

    def per_device(hidden, positions, gain_attn, gain_mlp, w_query, w_key, w_value, w_out, w_gate, w_up, w_down):
        num_layers = w_query.shape[0]
        head_dim = w_query.shape[3]
        cos_tab, sin_tab = rope_tables(positions, head_dim)
        pos_all = lax.all_gather(positions, "cp", tiled=True)
        key_list = []
        value_list = []
        for layer_idx in range(num_layers):
            normed = rms_norm(hidden, gain_attn[layer_idx])
            q_proj = jnp.einsum("td,dhe->the", normed, w_query[layer_idx], preferred_element_type=jnp.float32)
            queries = rotate_half(q_proj, cos_tab, sin_tab).astype(jnp.bfloat16)
            k_proj = jnp.einsum("td,dhe->the", normed, w_key[layer_idx], preferred_element_type=jnp.float32)
            key_local = rotate_half(k_proj, cos_tab, sin_tab).astype(jnp.bfloat16)
            value_local = jnp.einsum("td,dhe->the", normed, w_value[layer_idx], preferred_element_type=jnp.float32).astype(jnp.bfloat16)
            key_all = lax.all_gather(key_local, "cp", tiled=True)
            value_all = lax.all_gather(value_local, "cp", tiled=True)
            attn_out = attend(queries, key_all, value_all, positions, pos_all)
            attn_proj = jnp.einsum("the,hed->td", attn_out, w_out[layer_idx], preferred_element_type=jnp.float32)
            hidden = (hidden.astype(jnp.float32) + attn_proj).astype(jnp.bfloat16)
            normed_mlp = rms_norm(hidden, gain_mlp[layer_idx])
            gate_act = jnp.dot(normed_mlp, w_gate[layer_idx], preferred_element_type=jnp.float32)
            up_act = jnp.dot(normed_mlp, w_up[layer_idx], preferred_element_type=jnp.float32)
            mlp_hidden = (jax.nn.silu(gate_act) * up_act).astype(jnp.bfloat16)
            mlp_out = jnp.dot(mlp_hidden, w_down[layer_idx], preferred_element_type=jnp.float32)
            hidden = (hidden.astype(jnp.float32) + mlp_out).astype(jnp.bfloat16)
            key_list.append(key_local)
            value_list.append(value_local)
        key_heads = lax.all_to_all(jnp.stack(key_list), "cp", 2, 1, tiled=True)
        value_heads = lax.all_to_all(jnp.stack(value_list), "cp", 2, 1, tiled=True)
        return hidden, to_natural(key_heads, cp_size), to_natural(value_heads, cp_size)

    in_specs = (row_spec, pos_spec, rep_spec, rep_spec, rep_spec, rep_spec, rep_spec, rep_spec, rep_spec, rep_spec, rep_spec)
    return jax.shard_map(per_device, mesh=mesh, in_specs=in_specs, out_specs=(row_spec, cache_spec, cache_spec), check_vma=False)
```

profile of v0, /device:TPU:23, one launch (start us, length us, event | category | flops | bytes accessed | tf_op | source)
XLA Modules:
  0.0 435.9 jit_solution(2730351881559641705)
XLA Ops:
  7.3 1.5 slice_convert_fusion.1
  8.8 18.2 %fusion.210 = (bf16[1,2048,16,128]{3,2,1,0:T(8,128)(2,1)}, bf16[1,2048,16,128]{3,2,1,0:T(8,128)(2,1)}, bf16[1,2048,16,128]{3,2,1,0:T(8,128)(2,1)}) fusion(bf16[3,2048,16,128]{3,2,1,0:T(8,128)(2,1)} %param.15), kind=kLoop, calls=%fused_computation.200 | loop fusion | bytes 50331648 | tf_op jit(solution)/shard_map/slice | solution.py:69
  27.2 1.3 slice-done.2
  28.5 1.2 slice-done.3
  29.7 1.2 slice-done.4
  30.9 1.2 slice-done.5
  32.1 8.7 %fusion.211 = (bf16[1,2048,16,128]{3,2,1,0:T(8,128)(2,1)}, bf16[1,2048,16,128]{3,2,1,0:T(8,128)(2,1)}, bf16[1,2048,16,128]{3,2,1,0:T(8,128)(2,1)}) fusion(bf16[3,2048,16,128]{3,2,1,0:T(8,128)(2,1)S(1)} %bitcast.346), kind=kLoop, calls=%fused_computation.201 | loop fusion | bytes 50331648 | tf_op jit(solution)/shard_map/slice | solution.py:71
  40.8 5.2 %fusion.34 = f32[64,16,128]{2,0,1:T(8,128)S(1)} fusion(bf16[1,2048,16,128]{3,2,1,0:T(8,128)(2,1)} %get-tuple-element.5, bf16[64,2048]{1,0:T(8,128)(2,1)S(1)} %copy-done.6, f32[2048]{0:T(1024)S(1)} %bitcast.374, f32[64]{0:T(128)S(1)} %add_rsqrt_fusion.5), kind=kOutput, calls=%fused_computation.42 | convolution fusion | flops 537395200 | bytes 9183488 | tf_op jit(solution)/shard_map/td,dhe->the/dot_general | solution.py:69
  46.0 0.5 copy-done.3
  46.6 1.7 fusion.35
  48.5 0.4 subtract_convert_fusion.4
  48.9 0.9 pad_maximum_fusion.3
  49.9 14.6 %fusion.212 = (bf16[1,2048,16,128]{3,2,1,0:T(8,128)(2,1)}, bf16[1,2048,16,128]{3,2,1,0:T(8,128)(2,1)}, bf16[1,2048,16,128]{3,2,1,0:T(8,128)(2,1)S(1)}) fusion(bf16[3,2048,16,128]{3,2,1,0:T(8,128)(2,1)} %param.17), kind=kLoop, calls=%fused_computation.202 | loop fusion | bytes 50331648 | tf_op jit(solution)/shard_map/slice | solution.py:73
  64.6 2.4 fusion.147
  67.1 0.6 dynamic-slice
  68.6 16.3 %all-reduce = s32[1024]{0:T(1024)S(1)} all-reduce(s32[1024]{0:T(1024)S(1)} %dynamic-update-slice), channel_id=1, replica_groups=mesh['req'=4,'cp'=16] {'cp'}, use_global_device_ids=true, to_apply=%add | all-reduce | flops 1024 | bytes 8192
  85.1 7.7 %all-gather.9.cloned.1.call-done = bf16[1024,16,128]{2,0,1:T(8,128)(2,1)} async-done(((bf16[64,16,128]{2,0,1:T(8,128)(2,1)}), bf16[1024,16,128]{2,0,1:T(8,128)(2,1)}) %all-gather.9.cloned.1.call-update) | async-done | bytes 4194320 | tf_op jit(solution)/shard_map/all_gather | solution.py:74
  92.8 3.9 fusion.66
  96.7 2.0 copy-done.2
  98.7 1.1 fusion.63
  99.8 32.3 %all-gather.7.cloned.1.call-done = bf16[1024,16,128]{2,0,1:T(8,128)(2,1)} async-done(((bf16[64,16,128]{2,0,1:T(8,128)(2,1)}), bf16[1024,16,128]{2,0,1:T(8,128)(2,1)}) %all-gather.7.cloned.1.call-update) | async-done | bytes 4194320 | tf_op jit(solution)/shard_map/all_gather | solution.py:75
  132.1 7.5 %multiply_reduce_fusion.4 = (f32[64]{0:T(128)S(1)}, f32[64,2048]{1,0:T(8,128)S(1)}) fusion(bf16[3,16,128,2048]{3,2,1,0:T(8,128)(2,1)} %param.18, bf16[1024,16,128]{2,0,1:T(8,128)(2,1)} %all-gather.7.cloned.1.call-done, f32[16,64]{1,0:T(8,128)S(1)} %fusion.63, f32[16,1024,64]{1,2,0:T(8,128)} %copy-done.2, f32[16,64]{1,0:T(8,128)S(1)} %get-tuple-element.42, ...), kind=kOutput, calls=%fused_computation.148 | convolution fusion | flops 811466688 | bytes 17637632 | tf_op jit(solution)/shard_map/the,hed->td/dot_general | solution.py:77
  139.6 10.8 %fusion.16 = f32[64,5504]{1,0:T(8,128)} fusion(bf16[3,2048,5504]{2,1,0:T(8,128)(2,1)} %param.19, f32[64,2048]{1,0:T(8,128)S(1)} %get-tuple-element.45, f32[2048]{0:T(1024)S(1)} %bitcast.377, f32[64]{0:T(128)S(1)} %add_rsqrt_fusion.4), kind=kOutput, calls=%fused_computation.16 | convolution fusion | flops 1443233792 | bytes 24486144 | tf_op jit(solution)/shard_map/dot_general | solution.py:80
  150.4 11.3 %fusion.60 = bf16[64,5504]{1,0:T(8,128)(2,1)} fusion(bf16[3,2048,5504]{2,1,0:T(8,128)(2,1)} %param.20, f32[64,5504]{1,0:T(8,128)} %fusion.16, f32[64,2048]{1,0:T(8,128)S(1)} %get-tuple-element.45, f32[2048]{0:T(1024)S(1)} %bitcast.378, f32[64]{0:T(128)S(1)} %add_rsqrt_fusion.4), kind=kOutput, calls=%fused_computation.59 | convolution fusion | flops 1445347328 | bytes 25190656 | tf_op jit(solution)/shard_map/dot_general | solution.py:81
  161.7 10.0 %multiply_reduce_fusion.3 = (f32[64]{0:T(128)S(1)}, f32[64,2048]{1,0:T(8,128)S(1)}) fusion(f32[64,2048]{1,0:T(8,128)S(1)} %get-tuple-element.45, bf16[64,5504]{1,0:T(8,128)(2,1)} %fusion.60, bf16[3,5504,2048]{2,1,0:T(8,128)(2,1)} %param.21), kind=kOutput, calls=%fused_computation.146 | convolution fusion | flops 1443495936 | bytes 24297728 | tf_op jit(solution)/shard_map/dot_general | solution.py:83
  171.9 1.6 fusion.32
  173.6 1.6 fusion.31
  175.2 0.5 subtract_convert_fusion.2
  175.6 0.9 pad_maximum_fusion.4
  176.6 0.5 all-gather.11.cloned.1.call-start
  177.0 5.7 %fusion.148 = bf16[64,16,128]{2,0,1:T(8,128)(2,1)} fusion(bf16[64,2048,1]{1,0,2:T(8,128)(2,1)S(1)} %fusion.177, bf16[1,2048,16,128]{3,2,1,0:T(8,128)(2,1)} %get-tuple-element.10), kind=kOutput, calls=%fused_computation.114 | convolution fusion | flops 537001984 | bytes 8912896 | tf_op jit(solution)/shard_map/td,dhe->the/dot_general | solution.py:73
  182.9 30.7 %all-gather.13.cloned.1.call-done = bf16[1024,16,128]{2,0,1:T(8,128)(2,1)} async-done(((bf16[64,16,128]{2,0,1:T(8,128)(2,1)}), bf16[1024,16,128]{2,0,1:T(8,128)(2,1)}) %all-gather.13.cloned.1.call-update) | async-done | bytes 4194320 | tf_op jit(solution)/shard_map/all_gather | solution.py:74
  213.6 3.9 fusion.67
  217.5 2.0 copy-done.1
  219.5 1.1 fusion.64
  220.5 32.0 %all-gather.11.cloned.1.call-done = bf16[1024,16,128]{2,0,1:T(8,128)(2,1)} async-done(((bf16[64,16,128]{2,0,1:T(8,128)(2,1)}), bf16[1024,16,128]{2,0,1:T(8,128)(2,1)}) %all-gather.11.cloned.1.call-update) | async-done | bytes 4194320 | tf_op jit(solution)/shard_map/all_gather | solution.py:75
  252.6 7.5 %multiply_reduce_fusion.2 = (f32[64]{0:T(128)S(1)}, f32[64,2048]{1,0:T(8,128)S(1)}) fusion(f32[64,2048]{1,0:T(8,128)S(1)} %get-tuple-element.47, bf16[3,16,128,2048]{3,2,1,0:T(8,128)(2,1)} %param.18, bf16[1024,16,128]{2,0,1:T(8,128)(2,1)} %all-gather.11.cloned.1.call-done, f32[16,64]{1,0:T(8,128)S(1)} %fusion.64, f32[16,1024,64]{1,2,0:T(8,128)} %copy-done.1, ...), kind=kOutput, calls=%fused_computation.140 | convolution fusion | flops 811335616 | bytes 17899776 | tf_op jit(solution)/shard_map/the,hed->td/dot_general | solution.py:77
  260.1 0.8 copy-done.11
  260.9 10.8 %fusion.10 = f32[64,5504]{1,0:T(8,128)} fusion(bf16[3,2048,5504]{2,1,0:T(8,128)(2,1)} %param.19, f32[64,2048]{1,0:T(8,128)S(1)} %get-tuple-element.51, f32[2048]{0:T(1024)S(1)} %bitcast.372, f32[64]{0:T(128)S(1)} %add_rsqrt_fusion.2), kind=kOutput, calls=%fused_computation.10 | convolution fusion | flops 1443233792 | bytes 24486144 | tf_op jit(solution)/shard_map/dot_general | solution.py:80
  271.7 10.3 %fusion.57 = bf16[64,5504]{1,0:T(8,128)(2,1)S(1)} fusion(bf16[3,2048,5504]{2,1,0:T(8,128)(2,1)} %param.20, f32[64,5504]{1,0:T(8,128)} %fusion.10, f32[64,2048]{1,0:T(8,128)} %copy-done.11, f32[2048]{0:T(1024)S(1)} %bitcast.373, f32[64]{0:T(128)S(1)} %add_rsqrt_fusion.2), kind=kOutput, calls=%fused_computation.58 | convolution fusion | flops 1445347328 | bytes 25190656 | tf_op jit(solution)/shard_map/dot_general | solution.py:81
  282.0 9.9 %multiply_reduce_fusion.1 = (f32[64]{0:T(128)S(1)}, f32[64,2048]{1,0:T(8,128)S(1)}) fusion(f32[64,2048]{1,0:T(8,128)S(1)} %copy-done.12, bf16[64,5504]{1,0:T(8,128)(2,1)S(1)} %fusion.57, bf16[3,5504,2048]{2,1,0:T(8,128)(2,1)} %param.21), kind=kOutput, calls=%fused_computation.138 | convolution fusion | flops 1443495936 | bytes 24297728 | tf_op jit(solution)/shard_map/dot_general | solution.py:83
  292.0 1.6 fusion.29
  293.7 1.6 fusion.28
  295.3 0.5 subtract_convert_fusion
  295.8 0.9 pad_maximum_fusion.5
  296.9 5.8 %fusion.149 = bf16[64,16,128]{2,0,1:T(8,128)(2,1)} fusion(bf16[64,2048,1]{1,0,2:T(8,128)(2,1)S(1)} %fusion.178, bf16[1,2048,16,128]{3,2,1,0:T(8,128)(2,1)} %get-tuple-element.9), kind=kOutput, calls=%fused_computation.115 | convolution fusion | flops 537001984 | bytes 8912896 | tf_op jit(solution)/shard_map/td,dhe->the/dot_general | solution.py:73
  302.8 1.0 pad_maximum_fusion.1
  303.9 0.9 copy.37
  304.8 4.4 %all-to-all-start.1 = ((bf16[3,64,16,128]{3,1,0,2:T(8,128)(2,1)}), bf16[3,64,16,128]{3,1,0,2:T(8,128)(2,1)S(1)}, u32[]{:S(2)}, u32[]{:S(2)}) async-start(bf16[3,64,16,128]{3,1,0,2:T(8,128)(2,1)} %copy.37), calls=%async_computation.1 | async-start | bytes 1572864 | tf_op jit(solution)/shard_map/all_to_all | solution.py:88
  309.2 0.4 maximum_maximum_fusion
  309.6 0.9 copy.34
  310.6 27.4 %all-to-all-done.1 = bf16[3,64,16,128]{3,1,0,2:T(8,128)(2,1)S(1)} async-done(((bf16[3,64,16,128]{3,1,0,2:T(8,128)(2,1)}), bf16[3,64,16,128]{3,1,0,2:T(8,128)(2,1)S(1)}, u32[]{:S(2)}, u32[]{:S(2)}) %all-to-all-start.1) | async-done | bytes 786464 | tf_op jit(solution)/shard_map/all_to_all | solution.py:88
  338.0 5.1 %all-to-all-start = ((bf16[3,64,16,128]{3,1,0,2:T(8,128)(2,1)}), bf16[3,64,16,128]{3,1,0,2:T(8,128)(2,1)S(1)}, u32[]{:S(2)}, u32[]{:S(2)}) async-start(bf16[3,64,16,128]{3,1,0,2:T(8,128)(2,1)} %copy.34), calls=%async_computation | async-start | bytes 1572864 | tf_op jit(solution)/shard_map/all_to_all | solution.py:87
  343.3 0.9 copy.39
  344.2 21.1 %all-to-all-done = bf16[3,64,16,128]{3,1,0,2:T(8,128)(2,1)S(1)} async-done(((bf16[3,64,16,128]{3,1,0,2:T(8,128)(2,1)}), bf16[3,64,16,128]{3,1,0,2:T(8,128)(2,1)S(1)}, u32[]{:S(2)}, u32[]{:S(2)}) %all-to-all-start) | async-done | bytes 786464 | tf_op jit(solution)/shard_map/all_to_all | solution.py:87
  365.5 0.9 copy.36
  366.5 3.9 fusion.68
  370.4 2.0 copy-done
  372.4 1.1 fusion.65
  373.5 18.0 %all-gather.15.cloned.1.call-done = bf16[1024,16,128]{2,0,1:T(8,128)(2,1)} async-done(((bf16[64,16,128]{2,0,1:T(8,128)(2,1)}), bf16[1024,16,128]{2,0,1:T(8,128)(2,1)}) %all-gather.15.cloned.1.call-update) | async-done | bytes 4194320 | tf_op jit(solution)/shard_map/all_gather | solution.py:75
  391.4 7.5 %multiply_reduce_fusion = (f32[64]{0:T(128)S(1)}, f32[64,2048]{1,0:T(8,128)S(1)}) fusion(f32[64,2048]{1,0:T(8,128)S(1)} %get-tuple-element.53, bf16[3,16,128,2048]{3,2,1,0:T(8,128)(2,1)} %param.18, bf16[1024,16,128]{2,0,1:T(8,128)(2,1)} %all-gather.15.cloned.1.call-done, f32[16,64]{1,0:T(8,128)S(1)} %fusion.65, f32[16,1024,64]{1,2,0:T(8,128)} %copy-done, ...), kind=kOutput, calls=%fused_computation.132 | convolution fusion | flops 811335616 | bytes 17899776 | tf_op jit(solution)/shard_map/the,hed->td/dot_general | solution.py:77
  398.9 9.6 %fusion.4 = f32[64,5504]{1,0:T(8,128)S(1)} fusion(bf16[3,2048,5504]{2,1,0:T(8,128)(2,1)} %param.19, f32[64,2048]{1,0:T(8,128)S(1)} %get-tuple-element.57, f32[2048]{0:T(1024)S(1)} %bitcast.370, f32[64]{0:T(128)S(1)} %add_rsqrt_fusion), kind=kOutput, calls=%fused_computation.4 | convolution fusion | flops 1443233792 | bytes 24486144 | tf_op jit(solution)/shard_map/dot_general | solution.py:80
  408.6 10.0 %fusion.54 = bf16[64,5504]{1,0:T(8,128)(2,1)S(1)} fusion(bf16[3,2048,5504]{2,1,0:T(8,128)(2,1)} %param.20, f32[64,5504]{1,0:T(8,128)S(1)} %fusion.4, f32[64,2048]{1,0:T(8,128)S(1)} %get-tuple-element.57, f32[2048]{0:T(1024)S(1)} %bitcast.371, f32[64]{0:T(128)S(1)} %add_rsqrt_fusion), kind=kOutput, calls=%fused_computation.57 | convolution fusion | flops 1445347328 | bytes 25190656 | tf_op jit(solution)/shard_map/dot_general | solution.py:81
  418.5 10.4 %fusion.96 = bf16[64,2048]{1,0:T(8,128)(2,1)} fusion(f32[64,2048]{1,0:T(8,128)S(1)} %get-tuple-element.57, bf16[64,5504]{1,0:T(8,128)(2,1)S(1)} %fusion.54, bf16[3,5504,2048]{2,1,0:T(8,128)(2,1)} %param.21), kind=kOutput, calls=%fused_computation.84 | convolution fusion | flops 1443102720 | bytes 24035328 | tf_op jit(solution)/shard_map/dot_general | solution.py:83
  (84 shorter events, 2.2 us)
Async XLA Ops:
  7.2 85.6 %all-gather.9.cloned.1.call-start = ((), (), s32[]{:S(2)}) async-start(), calls=%async_computation.3 | async-start | bytes 4456448 | tf_op jit(solution)/shard_map/all_gather | solution.py:74
  7.3 20.0 %slice-start = ((s8[25165824]{0:T(1024)(128)(4,1)}), s8[4194304]{0:T(1024)(128)(4,1)S(1)}, s32[]{:S(2)}) async-start(s8[25165824]{0:T(1024)(128)(4,1)} %bitcast.345), calls=%async_computation.8 | async-start | bytes 8388608
  8.8 18.3 %copy-start.6 = (bf16[64,2048]{1,0:T(8,128)(2,1)S(1)}, bf16[64,2048]{1,0:T(8,128)(2,1)}, u32[]{:S(2)}) copy-start(bf16[64,2048]{1,0:T(8,128)(2,1)} %param.11) | copy-start | bytes 786436
  8.8 18.4 %slice-start.1 = ((s8[25165824]{0:T(1024)(128)(4,1)}), s8[4194304]{0:T(1024)(128)(4,1)S(1)}, s32[]{:S(2)}) async-start(s8[25165824]{0:T(1024)(128)(4,1)} %bitcast.345), calls=%async_computation.9 | async-start | bytes 8388608
  8.8 19.7 %slice-start.2 = ((s8[25165824]{0:T(1024)(128)(4,1)}), s8[4194304]{0:T(1024)(128)(4,1)S(1)}, s32[]{:S(2)}) async-start(s8[25165824]{0:T(1024)(128)(4,1)} %bitcast.345), calls=%async_computation.10 | async-start | bytes 8388608
  8.8 20.9 %slice-start.3 = ((s8[25165824]{0:T(1024)(128)(4,1)}), s8[4194304]{0:T(1024)(128)(4,1)S(1)}, s32[]{:S(2)}) async-start(s8[25165824]{0:T(1024)(128)(4,1)} %bitcast.345), calls=%async_computation.11 | async-start | bytes 8388608
  8.8 22.1 %slice-start.4 = ((s8[25165824]{0:T(1024)(128)(4,1)}), s8[4194304]{0:T(1024)(128)(4,1)S(1)}, s32[]{:S(2)}) async-start(s8[25165824]{0:T(1024)(128)(4,1)} %bitcast.345), calls=%async_computation.12 | async-start | bytes 8388608
  8.8 23.3 %slice-start.5 = ((s8[25165824]{0:T(1024)(128)(4,1)}), s8[4194304]{0:T(1024)(128)(4,1)S(1)}, s32[]{:S(2)}) async-start(s8[25165824]{0:T(1024)(128)(4,1)} %bitcast.345), calls=%async_computation.13 | async-start | bytes 8388608
  40.8 5.8 %copy-start.3 = (bf16[1,2048,16,128]{3,2,1,0:T(8,128)(2,1)S(1)}, bf16[1,2048,16,128]{3,2,1,0:T(8,128)(2,1)}, u32[]{:S(2)}) copy-start(bf16[1,2048,16,128]{3,2,1,0:T(8,128)(2,1)} %get-tuple-element.8) | copy-start | bytes 25165828
  46.6 1.7 copy-start.9
  49.9 82.2 %all-gather.7.cloned.1.call-start = ((), (), s32[]{:S(2)}) async-start(), calls=%async_computation.2 | async-start | bytes 4456448 | tf_op jit(solution)/shard_map/all_gather | solution.py:75
  64.6 2.6 copy-start.10
  64.6 20.5 %copy-start.7 = (bf16[3,2048]{1,0:T(4,128)(2,1)S(1)}, bf16[3,2048]{1,0:T(4,128)(2,1)}, u32[]{:S(2)}) copy-start(bf16[3,2048]{1,0:T(4,128)(2,1)} %param.14) | copy-start | bytes 36868
  67.1 146.6 %all-gather.13.cloned.1.call-start = ((), (), s32[]{:S(2)}) async-start(), calls=%async_computation.5 | async-start | bytes 4456448 | tf_op jit(solution)/shard_map/all_gather | solution.py:74
  96.7 2.1 copy-start.2
  139.6 32.3 %slice-start.12 = ((s8[8388608]{0:T(1024)(128)(4,1)}), s8[4194304]{0:T(1024)(128)(4,1)S(1)}, s32[]{:S(2)}) async-start(s8[8388608]{0:T(1024)(128)(4,1)} %bitcast.353), calls=%async_computation.20 | async-start | bytes 8388608
  150.4 21.5 %slice-start.13 = ((s8[8388608]{0:T(1024)(128)(4,1)}), s8[4194304]{0:T(1024)(128)(4,1)S(1)}, s32[]{:S(2)}) async-start(s8[8388608]{0:T(1024)(128)(4,1)} %bitcast.353), calls=%async_computation.21 | async-start | bytes 8388608
  150.4 23.1 %slice-start.10 = ((s8[8388608]{0:T(1024)(128)(4,1)}), s8[4194304]{0:T(1024)(128)(4,1)S(1)}, s32[]{:S(2)}) async-start(s8[8388608]{0:T(1024)(128)(4,1)} %bitcast.351), calls=%async_computation.18 | async-start | bytes 8388608
  161.7 11.8 %slice-start.11 = ((s8[8388608]{0:T(1024)(128)(4,1)}), s8[4194304]{0:T(1024)(128)(4,1)S(1)}, s32[]{:S(2)}) async-start(s8[8388608]{0:T(1024)(128)(4,1)} %bitcast.351), calls=%async_computation.19 | async-start | bytes 8388608
  176.6 76.0 %all-gather.11.cloned.1.call-start = ((), (), s32[]{:S(2)}) async-start(), calls=%async_computation.4 | async-start | bytes 4456448 | tf_op jit(solution)/shard_map/all_gather | solution.py:75
  182.8 183.6 %all-gather.17.cloned.1.call-start = ((), (), s32[]{:S(2)}) async-start(), calls=%async_computation.7 | async-start | bytes 4456448 | tf_op jit(solution)/shard_map/all_gather | solution.py:74
  217.5 2.0 copy-start.1
  260.1 0.8 copy-start.11
  260.9 31.1 %slice-start.8 = ((s8[8388608]{0:T(1024)(128)(4,1)}), s8[4194304]{0:T(1024)(128)(4,1)S(1)}, s32[]{:S(2)}) async-start(s8[8388608]{0:T(1024)(128)(4,1)} %bitcast.349), calls=%async_computation.16 | async-start | bytes 8388608
  271.7 10.3 %copy-start.12 = (f32[64,2048]{1,0:T(8,128)S(1)}, f32[64,2048]{1,0:T(8,128)}, u32[]{:S(2)}) copy-start(f32[64,2048]{1,0:T(8,128)} %copy-done.11) | copy-start | bytes 1572868
  271.7 20.3 %slice-start.9 = ((s8[8388608]{0:T(1024)(128)(4,1)}), s8[4194304]{0:T(1024)(128)(4,1)S(1)}, s32[]{:S(2)}) async-start(s8[8388608]{0:T(1024)(128)(4,1)} %bitcast.349), calls=%async_computation.17 | async-start | bytes 8388608
  271.7 22.0 %slice-start.6 = ((s8[8388608]{0:T(1024)(128)(4,1)}), s8[4194304]{0:T(1024)(128)(4,1)S(1)}, s32[]{:S(2)}) async-start(s8[8388608]{0:T(1024)(128)(4,1)} %bitcast.347), calls=%async_computation.14 | async-start | bytes 8388608
  281.9 9.9 %copy-start.8 = (f32[1,2048]{1,0:T(1,128)S(1)}, f32[1,2048]{1,0:T(1,128)}, u32[]{:S(2)}) copy-start(f32[1,2048]{1,0:T(1,128)} %get-tuple-element.37) | copy-start | bytes 24580
  282.0 11.7 %slice-start.7 = ((s8[8388608]{0:T(1024)(128)(4,1)}), s8[4194304]{0:T(1024)(128)(4,1)S(1)}, s32[]{:S(2)}) async-start(s8[8388608]{0:T(1024)(128)(4,1)} %bitcast.347), calls=%async_computation.15 | async-start | bytes 8388608
  296.7 94.8 %all-gather.15.cloned.1.call-start = ((), (), s32[]{:S(2)}) async-start(), calls=%async_computation.6 | async-start | bytes 4456448 | tf_op jit(solution)/shard_map/all_gather | solution.py:75
  296.9 5.9 %copy-start.4 = (bf16[64,16,128]{2,0,1:T(8,128)(2,1)S(1)}, bf16[64,16,128]{2,0,1:T(8,128)(2,1)}, u32[]{:S(2)}) copy-start(bf16[64,16,128]{2,0,1:T(8,128)(2,1)} %fusion.147) | copy-start | bytes 786436
  296.9 5.9 %copy-start.5 = (bf16[64,16,128]{2,0,1:T(8,128)(2,1)S(1)}, bf16[64,16,128]{2,0,1:T(8,128)(2,1)}, u32[]{:S(2)}) copy-start(bf16[64,16,128]{2,0,1:T(8,128)(2,1)} %fusion.148) | copy-start | bytes 786436
  304.8 33.2 %all-to-all-start.1 = ((bf16[3,64,16,128]{3,1,0,2:T(8,128)(2,1)}), bf16[3,64,16,128]{3,1,0,2:T(8,128)(2,1)S(1)}, u32[]{:S(2)}, u32[]{:S(2)}) async-start(bf16[3,64,16,128]{3,1,0,2:T(8,128)(2,1)} %copy.37), calls=%async_computation.1 | async-start | bytes 1572864 | tf_op jit(solution)/shard_map/all_to_all | solution.py:88
  338.0 27.3 %all-to-all-start = ((bf16[3,64,16,128]{3,1,0,2:T(8,128)(2,1)}), bf16[3,64,16,128]{3,1,0,2:T(8,128)(2,1)S(1)}, u32[]{:S(2)}, u32[]{:S(2)}) async-start(bf16[3,64,16,128]{3,1,0,2:T(8,128)(2,1)} %copy.34), calls=%async_computation | async-start | bytes 1572864 | tf_op jit(solution)/shard_map/all_to_all | solution.py:87
  370.4 2.0 copy-start
Sparse Core Ops, SparseCore 0:
  50.0 42.7 all-gather.8
  95.0 37.0 all-gather.6
  176.7 36.8 all-gather.12
  215.7 36.8 all-gather.10
  296.8 52.0 all-gather.16
  350.4 40.9 all-gather.14
where the time goes:
time: 444 us; the launch traced here: 436 us
  waiting for transfers between devices  170 us (38%)
  matrix products  154 us (35%)
  local copies, waits for them, and re-layouts  58.7 us (13%)
  blocking collectives  16.3 us (4%)
  between operations  15.5 us (3%)
  other arithmetic  11 us (2%)
  starting transfers between devices  10.5 us (2%)
    all_gather x3, waiting for transfers between devices, per_device(): value_all = lax.all_gather(value_local, 'cp', tiled=True)  82.3 us
    all_gather x3, waiting for transfers between devices, per_device(): key_all = lax.all_gather(key_local, 'cp', tiled=True)  38.4 us
    dot_general x3, matrix products, per_device(): jnp.dot(normed_mlp, w_up[layer_idx], preferred_element_type=jnp.float32)  31.5 us
    dot_general x3, matrix products, per_device(): jnp.dot(normed_mlp, w_gate[layer_idx], preferred_element_type=jnp.float32)  31.2 us
    dot_general x3, matrix products, per_device(): jnp.dot(mlp_hidden, w_down[layer_idx], preferred_element_type=jnp.float32)  30.2 us
    all_to_all x1, waiting for transfers between devices, per_device(): value_heads = lax.all_to_all(jnp.stack(value_list), 'cp', 2, 1, tiled=True)  27.4 us
    dot_general x3, matrix products, per_device(): jnp.einsum('the,hed->td', attn_out, w_out[layer_idx], preferred_element_t...  22.4 us
    all_to_all x1, waiting for transfers between devices, per_device(): key_heads = lax.all_to_all(jnp.stack(key_list), 'cp', 2, 1, tiled=True)  21.1 us
  transfers between devices with their start and end apart: 8, of which 7 were waited for; matrix products, arithmetic and copies ran while one was open for 11% of the time, Pallas kernels for 0%

commit v1 on v0

v1 whole, which is shorter than its diff:
```python
import functools

import jax
import jax.numpy as jnp
from jax import lax
from jax.experimental import pallas as pl
from jax.experimental.pallas import tpu as pltpu
from jax.sharding import PartitionSpec as P

NORM_EPS = 1e-5
ROPE_BASE = 10000.0
F32 = jnp.float32
BF16 = jnp.bfloat16


def rope_tables(pos_vec, head_dim):
    inv_freq = ROPE_BASE ** (-jnp.arange(0, head_dim, 2, dtype=F32) / head_dim)
    angles = pos_vec.astype(F32)[..., None] * inv_freq
    cos_tab, sin_tab = jnp.cos(angles), jnp.sin(angles)
    return jnp.stack([jnp.concatenate([cos_tab, cos_tab], -1), jnp.concatenate([-sin_tab, sin_tab], -1)])


def dot(a, b):
    return jnp.dot(a, b, preferred_element_type=F32)


def kernel(cfg, x_in, cs_in, ga, gm, wq, wk, wv, wo, wg, wu, wd, x_out, kc, vc,
           xs, tab, ha, hb, acc, stage, nat, onat, orecv, act, pfull, precv, lg,
           bqkv, bo, bg, bu, bd, wsem, csem, tsend, trecv, hsend, hrecv, psend, precvs,
           qsend, qrecv, osend, orecvs):
    cp, n_layers, half, seq, heads, hd, dim, fw, foff = cfg
    seg = 2 * half
    nseg = seq // seg
    hpc = heads // 2
    me = lax.axis_index("cp")
    core = lax.rem(me, 2)
    chip = me // 2
    partner = me + 1 - 2 * core

    def al(v, m):
        return pl.multiple_of(v, m)

    my_rows = (al(half * core, half), al(seg + half * (1 - core), half))
    pa_rows = (al(half * (1 - core), half), al(seg + half * core, half))
    hbase = al(hpc * core, hpc)

    def rcopy(src, dst, ss, rs, dev):
        return pltpu.make_async_remote_copy(src_ref=src, dst_ref=dst, send_sem=ss, recv_sem=rs,
                                            device_id={"cp": dev}, device_id_type=pl.DeviceIdType.MESH)

    qkv_hbm = (wk, wq, wv)

    def w_copy(l, i):
        fo = al(core * foff, 128)
        if i < 3:
            src, dst = qkv_hbm[i].at[l, :, pl.ds(hbase, hpc), :], bqkv.at[i]
        elif i == 3:
            src, dst = wo.at[l, pl.ds(hbase, hpc)], bo
        elif i < 6:
            src, dst = (wg, wu)[i - 4].at[l, :, pl.ds(fo, fw)], (bg, bu)[i - 4]
        else:
            src, dst = wd.at[l, pl.ds(fo, fw), :], bd
        return pltpu.make_async_copy(src, dst, wsem.at[i])

    for i in range(7):
        w_copy(0, i).start()

    barrier = pltpu.get_barrier_semaphore()
    for d in range(1, cp):
        pl.semaphore_signal(barrier, inc=1, device_id={"cp": lax.rem(me + d, cp)}, device_id_type=pl.DeviceIdType.MESH)
    pl.semaphore_wait(barrier, cp - 1)

    tcp = [rcopy(cs_in.at[:, pl.ds(half * i, half), :], tab.at[:, pl.ds(my_rows[i], half), :], tsend.at[i], trecv.at[i], partner)
           for i in range(2)]
    for c in tcp:
        c.start()
    for i in range(2):
        for r in range(2):
            tab[r, pl.ds(my_rows[i], half), :] = cs_in[r, half * i:half * (i + 1), :]
    xs[...] = x_in[...].astype(F32)

    def norm_exchange(gain, hbuf):
        xv = xs[...]
        inv = lax.rsqrt(jnp.mean(xv * xv, axis=-1, keepdims=True) + NORM_EPS)
        hv = (xv * inv * gain.astype(F32)).astype(BF16)
        for i in range(2):
            hbuf[pl.ds(my_rows[i], half), :] = hv[half * i:half * (i + 1)]
        cps = [rcopy(hbuf.at[pl.ds(my_rows[i], half), :], hbuf.at[pl.ds(my_rows[i], half), :], hsend.at[i], hrecv.at[i], partner)
               for i in range(2)]
        for c in cps:
            c.start()
        for i in range(2):
            rcopy(hbuf.at[pl.ds(pa_rows[i], half), :], hbuf.at[pl.ds(pa_rows[i], half), :], hsend.at[i], hrecv.at[i], partner).wait_recv()
        for c in cps:
            c.wait_send()

    ncol = dim // 4

    def partial_exchange(product):
        def body(i, _):
            cols = pl.ds(al(i * ncol, ncol), ncol)
            pfull[:, cols] = product(cols)
            for r in range(2):
                rcopy(pfull.at[pl.ds(pa_rows[r], half), cols], precv.at[pl.ds(half * r, half), cols],
                      psend.at[i, r], precvs.at[i, r], partner).start()
            return 0
        lax.fori_loop(0, 4, body, 0)

        def done(i, _):
            cols = pl.ds(al(i * ncol, ncol), ncol)
            for r in range(2):
                rcopy(pfull.at[pl.ds(pa_rows[r], half), cols], precv.at[pl.ds(half * r, half), cols],
                      psend.at[i, r], precvs.at[i, r], partner).wait()
            for r in range(2):
                rows = slice(half * r, half * (r + 1))
                s = pfull[pl.ds(my_rows[r], half), cols] + precv[rows, cols]
                xs[rows, cols] = (xs[rows, cols] + s).astype(BF16).astype(F32)
            return 0
        lax.fori_loop(0, 4, done, 0)

    src_core = me // hpc
    my_col = lax.rem(me, hpc)

    def layer(l, _):
        par = lax.rem(l, 2)
        more = l + 1 < n_layers

        def prefetch(i):
            @pl.when(more)
            def _():
                w_copy(l + 1, i).start()

        norm_exchange(ga[l], ha)

        @pl.when(l == 0)
        def _():
            for i in range(2):
                rcopy(cs_in.at[:, pl.ds(half * i, half), :], tab.at[:, pl.ds(pa_rows[i], half), :],
                      tsend.at[i], trecv.at[i], partner).wait()

        for t in range(3):
            w_copy(l, t).wait()
            acc[...] = dot(ha[...], bqkv[t].reshape(dim, hpc * hd))
            prefetch(t)
            for j in range(hpc):
                a = acc[:, hd * j:hd * (j + 1)]
                if t < 2:
                    a = a * tab[0] + pltpu.roll(a, hd // 2, 1) * tab[1]
                stage[t, j] = a.astype(BF16)
            for j in range(hpc):
                n = hbase + j
                segs = (chip, nseg - 1 - chip)

                @pl.when(n != me)
                def _():
                    for r in range(2):
                        rcopy(stage.at[t, j, pl.ds(seg * r, seg), :], nat.at[par, t, pl.ds(al(segs[r] * seg, seg), seg), :],
                              qsend.at[t, j, r], qrecv.at[par, t, segs[r]], n).start()

                @pl.when(n == me)
                def _():
                    for r in range(2):
                        nat[par, t, pl.ds(al(segs[r] * seg, seg), seg), :] = stage[t, j, seg * r:seg * (r + 1), :]

        def wait_nat(t):
            for s in range(nseg):
                src = 2 * min(s, nseg - 1 - s) + src_core

                @pl.when(src != me)
                def _():
                    rcopy(stage.at[t, 0, pl.ds(0, seg), :], nat.at[par, t, pl.ds(s * seg, seg), :],
                          qsend.at[t, 0, 0], qrecv.at[par, t, s], src).wait_recv()

        def cache_copy(i):
            return pltpu.make_async_copy(nat.at[par, 2 * i], (kc, vc)[i].at[l], csem.at[i])

        wait_nat(0)
        cache_copy(0).start()
        wait_nat(1)
        wait_nat(2)
        cache_copy(1).start()

        qb = 256
        for b in range(seq // qb):
            n_keys = qb * (b + 1)
            q = nat[par, 1, pl.ds(qb * b, qb), :]
            k = nat[par, 0, pl.ds(0, n_keys), :]
            s = lax.dot_general(q, k, (((1,), (1,)), ((), ())), preferred_element_type=F32) * (hd ** -0.5)
            rows = lax.broadcasted_iota(jnp.int32, (qb, n_keys), 0) + qb * b
            cols = lax.broadcasted_iota(jnp.int32, (qb, n_keys), 1)
            s = jnp.where(cols <= rows, s, -jnp.inf)
            e = jnp.exp(s - jnp.max(s, axis=-1, keepdims=True))
            p = (e / jnp.sum(e, axis=-1, keepdims=True)).astype(BF16)
            onat[pl.ds(qb * b, qb), :] = dot(p, nat[par, 2, pl.ds(0, n_keys), :]).astype(BF16)
            for s_i in range(b * qb // seg, (b + 1) * qb // seg):
                r = 1 if s_i >= nseg // 2 else 0
                dest = 2 * min(s_i, nseg - 1 - s_i) + src_core
                cols_o = pl.ds(al(my_col * hd, hd), hd)

                @pl.when(dest != me)
                def _():
                    rcopy(onat.at[pl.ds(s_i * seg, seg), :], orecv.at[pl.ds(seg * r, seg), cols_o],
                          osend.at[s_i], orecvs.at[my_col, r], dest).start()

                @pl.when(dest == me)
                def _():
                    orecv[pl.ds(seg * r, seg), cols_o] = onat[s_i * seg:(s_i + 1) * seg, :]

        for j in range(hpc):
            @pl.when(hbase + j != me)
            def _():
                for r in range(2):
                    rcopy(onat.at[pl.ds(0, seg), :], orecv.at[pl.ds(seg * r, seg), pl.ds(hd * j, hd)],
                          osend.at[0], orecvs.at[j, r], hbase + j).wait_recv()

        w_copy(l, 3).wait()
        partial_exchange(lambda cols: dot(orecv[...], bo[:, :, cols].reshape(hpc * hd, ncol)))
        prefetch(3)
        norm_exchange(gm[l], hb)
        w_copy(l, 4).wait()
        w_copy(l, 5).wait()
        fc = 256

        def mlp(i, _):
            cols = pl.ds(al(i * fc, fc), fc)
            g = dot(hb[...], bg[:, cols])
            u = dot(hb[...], bu[:, cols])
            a = (jax.nn.silu(g) * u).astype(BF16)
            cid = lax.broadcasted_iota(jnp.int32, (2 * seg, fc), 1) + i * fc
            act[:, cols] = jnp.where(cid >= core * (fw - foff), a, jnp.zeros_like(a))
            return 0
        lax.fori_loop(0, fw // fc, mlp, 0)
        prefetch(4)
        prefetch(5)
        w_copy(l, 6).wait()
        partial_exchange(lambda cols: dot(act[...], bd[:, cols]))
        prefetch(6)

        for i in range(2):
            cache_copy(i).wait()
        for t in range(3):
            for j in range(hpc):
                @pl.when(hbase + j != me)
                def _():
                    for r in range(2):
                        rcopy(stage.at[t, j, pl.ds(seg * r, seg), :], nat.at[par, t, pl.ds(0, seg), :],
                              qsend.at[t, j, r], qrecv.at[par, t, 0], hbase + j).wait_send()
        for s_i in range(nseg):
            dest = 2 * min(s_i, nseg - 1 - s_i) + src_core

            @pl.when(dest != me)
            def _():
                rcopy(onat.at[pl.ds(s_i * seg, seg), :], orecv.at[pl.ds(0, seg), pl.ds(0, hd)],
                      osend.at[s_i], orecvs.at[0, 0], dest).wait_send()
        return 0

    lax.fori_loop(0, n_layers, layer, 0)
    x_out[...] = xs[...].astype(BF16)


def solution(mesh):
    cp = mesh.shape["cp"]
    row_spec = P(("req", "cp"), None)
    rep = P()
    cache_spec = P(None, "req", "cp", None)

    def per_device(hidden, positions, ga, gm, wq, wk, wv, wo, wg, wu, wd):
        rows, dim = hidden.shape
        n_layers, _, heads, hd = wq.shape
        ff = wg.shape[2]
        seq = rows * cp
        half = rows // 2
        seg = rows
        nseg = seq // seg
        hpc = heads // 2
        tiles = ff // 128
        fw = -(-tiles // 4) * 2 * 128
        foff = ff - fw
        cfg = (cp, n_layers, half, seq, heads, hd, dim, fw, foff)
        cs = rope_tables(positions, hd)
        vm = pl.BlockSpec(memory_space=pltpu.VMEM)
        hb = pl.BlockSpec(memory_space=pltpu.HBM)
        dma = pltpu.SemaphoreType.DMA
        V = pltpu.VMEM
        x, kc, vc = pl.pallas_call(
            functools.partial(kernel, cfg),
            out_shape=(jax.ShapeDtypeStruct((rows, dim), BF16),
                       jax.ShapeDtypeStruct((n_layers, seq, hd), BF16),
                       jax.ShapeDtypeStruct((n_layers, seq, hd), BF16)),
            in_specs=[vm] * 4 + [hb] * 7,
            out_specs=(vm, hb, hb),
            scratch_shapes=[
                V((rows, dim), F32), V((2, 2 * seg, hd), F32), V((2 * seg, dim), BF16), V((2 * seg, dim), BF16),
                V((2 * seg, hpc * hd), F32), V((3, hpc, 2 * seg, hd), BF16), V((2, 3, seq, hd), BF16), V((seq, hd), BF16),
                V((2 * seg, hpc * hd), BF16), V((2 * seg, fw), BF16), V((2 * seg, dim), F32), V((rows, dim), F32), V((8, 128), F32),
                V((3, dim, hpc, hd), BF16), V((hpc, hd, dim), BF16), V((dim, fw), BF16), V((dim, fw), BF16), V((fw, dim), BF16),
                dma((7,)), dma((2,)), dma((2,)), dma((2,)), dma((2,)), dma((2,)), dma((4, 2)), dma((4, 2)),
                dma((3, hpc, 2)), dma((2, 3, nseg)), dma((nseg,)), dma((hpc, 2)),
            ],
            compiler_params=pltpu.CompilerParams(collective_id=0, has_side_effects=True, vmem_limit_bytes=67043328),
            name="prefill",
        )(hidden, cs, ga.reshape(n_layers, 1, dim), gm.reshape(n_layers, 1, dim), wq, wk, wv, wo, wg, wu, wd)
        return x, kc.reshape(n_layers, seq, 1, hd), vc.reshape(n_layers, seq, 1, hd)

    in_specs = (row_spec, P(("req", "cp"))) + (rep,) * 9
    return jax.shard_map(per_device, mesh=mesh, in_specs=in_specs, out_specs=(row_spec, cache_spec, cache_spec), check_vma=False)
```

time: 444 us -> 162 us (0.36); the launches traced: 436 us -> 161 us
  waiting for transfers between devices: 170 us -> 0 us
  matrix products: 154 us -> 0 us
  Pallas kernels: 0 us -> 150 us
  local copies, waits for them, and re-layouts: 58.7 us -> 8.49 us
  blocking collectives: 16.3 us -> 0 us
  between operations: 15.5 us -> 0.66 us
  starting transfers between devices: 10.5 us -> 0 us
  other arithmetic: 11 us -> 1.58 us
    dot_general x24 -> x0, matrix products: 154 us -> none  [the longest x3 31.5 us: per_device(): jnp.dot(normed_mlp, w_up[layer_idx], preferred_element_type=jnp.float32)]
    pallas_call x0 -> x1, Pallas kernels: none -> 150 us  [per_device(): pl.pallas_call(functools.partial(kernel, cfg), out_shape=(jax.ShapeDtypeS...]
    all_gather x6 -> x0, waiting for transfers between devices: 121 us -> none  [the longest x3 82.3 us: per_device(): value_all = lax.all_gather(value_local, 'cp', tiled=True)]
    all_to_all x2 -> x0, waiting for transfers between devices: 48.5 us -> none  [the longest x1 27.4 us: per_device(): value_heads = lax.all_to_all(jnp.stack(value_list), 'cp', 2, 1, tiled=True)]
    slice x3 -> x0, local copies, waits for them, and re-layouts: 41.6 us -> none  [the longest x1 18.2 us: per_device(): w_query[layer_idx]]
    unnamed x1 -> x0, blocking collectives: 16.3 us -> none
    all_to_all x2 -> x0, starting transfers between devices: 9.51 us -> none  [the longest x1 5.12 us: per_device(): key_heads = lax.all_to_all(jnp.stack(key_list), 'cp', 2, 1, tiled=True)]
    unnamed x57 -> x3, local copies, waits for them, and re-layouts: 13.1 us -> 5.79 us
  transfers between devices with their start and end apart: 8 -> 0, of which waited for: 7 -> 0; matrix products, arithmetic and copies ran while one was open for 11% -> 0% of each run, Pallas kernels for 0% -> 0%
where the time goes in v1:
time: 162 us; the launch traced here: 161 us
  Pallas kernels  150 us (93%)
  local copies, waits for them, and re-layouts  8.49 us (5%)
    pallas_call x1, Pallas kernels, per_device(): pl.pallas_call(functools.partial(kernel, cfg), out_shape=(jax.ShapeDtypeS...  150 us
    unnamed x3, local copies, waits for them, and re-layouts  5.79 us

profile of v1, /device:TPU:23, one launch (start us, length us, event | category | flops | bytes accessed | tf_op | source)
XLA Modules:
  0.0 161.2 jit_solution(10693827612380043986)
XLA Ops:
  0.6 0.7 convert_element_type.3
  1.3 1.4 copy.16.ga
  2.7 1.3 copy.17.gm
  4.0 0.2 multiply_cosine_fusion
  4.2 0.1 maximum_bitcast_fusion
  4.3 0.6 pad_maximum_fusion.cs_in
  4.9 150.4 %prefill.1 = (bf16[64,2048]{1,0:T(8,128)(2,1)}, bf16[3,1024,128]{2,1,0:T(8,128)(2,1)}, bf16[3,1024,128]{2,1,0:T(8,128)(2,1)}) custom-call(bf16[64,2048]{1,0:T(8,128)(2,1)} %x_in.1, f32[2,64,128]{2,1,0:T(8,128)} %pad_maximum_fusion.cs_in, bf16[3,1,2048]{2,1,0:T(2,128)(2,1)} %copy.16.ga, bf16[3,1,2048]{2,1,0:T(2,128)(2,1)} %copy.17.gm, ...), custom_call_target="tpu_custom_call" | custom-call | tf_op jit(solution)/shard_map/prefill/pallas_call | solution.py:285
  155.4 1.7 %copy.23 = bf16[64,2048]{1,0:T(8,128)(2,1)} copy(bf16[64,2048]{1,0:T(8,128)(2,1)} %get-tuple-element.23) | data formatting | bytes 524288
  157.1 2.1 %copy.24 = bf16[3,1024,1,128]{3,1,2,0:T(8,128)(2,1)} copy(bf16[3,1024,1,128]{3,1,2,0:T(8,128)(2,1)} %bitcast.13) | data formatting | bytes 1572864
  159.1 2.1 %copy.25 = bf16[3,1024,1,128]{3,1,2,0:T(8,128)(2,1)} copy(bf16[3,1024,1,128]{3,1,2,0:T(8,128)(2,1)} %bitcast.12) | data formatting | bytes 1572864
  (1 shorter events, 0.0 us)

commit v2 on v1

v2 whole, which is shorter than its diff:
```python
import functools

import jax
import jax.numpy as jnp
from jax import lax
from jax.experimental import pallas as pl
from jax.experimental.pallas import tpu as pltpu
from jax.sharding import PartitionSpec as P

NORM_EPS = 1e-5
ROPE_BASE = 10000.0
F32 = jnp.float32
BF16 = jnp.bfloat16


def rope_tables(pos_vec, head_dim):
    inv_freq = ROPE_BASE ** (-jnp.arange(0, head_dim, 2, dtype=F32) / head_dim)
    angles = pos_vec.astype(F32)[..., None] * inv_freq
    cos_tab, sin_tab = jnp.cos(angles), jnp.sin(angles)
    return cos_tab, sin_tab


def dot(a, b):
    return jnp.dot(a, b, preferred_element_type=F32)


def kernel(cfg, x_in, cos_in, sin_in, ga, gm, wq, wk, wv, wo, wg, wu, wd, x_out, kc, vc,
           xs, gains, tab, hbuf, act, stage, nat, onat, probs, orecv, pfull, precv,
           bqkv, bo, bg, bu, bd, wsem, csem, isend, irecv, psend, precvs,
           qsend, qrecv, osend, orecvs):
    cp, n_layers, half, seq, heads, hd, dim, fw, foff = cfg
    seg = 2 * half
    nseg = seq // seg
    hpc = heads // 2
    nchip = cp // 2
    me = lax.axis_index("cp")
    core = lax.rem(me, 2)
    chip = me // 2
    partner = me + 1 - 2 * core

    def al(v, m):
        return pl.multiple_of(v, m)

    my_rows = (al(half * core, half), al(seg + half * (1 - core), half))
    pa_rows = (al(half * (1 - core), half), al(seg + half * core, half))
    hbase = al(hpc * lax.rem(core + chip + chip // (nchip // 2), 2), hpc)
    my_half = me // hpc
    my_col = lax.rem(me, hpc)

    def worker(z):
        return 2 * z + lax.rem(my_half + z + z // (nchip // 2), 2)

    def rcopy(src, dst, ss, rs, dev):
        return pltpu.make_async_remote_copy(src_ref=src, dst_ref=dst, send_sem=ss, recv_sem=rs,
                                            device_id={"cp": dev}, device_id_type=pl.DeviceIdType.MESH)

    qkv_hbm = (wk, wq, wv)

    def w_copy(l, i):
        fo = al(core * foff, 128)
        if i < 3:
            src, dst = qkv_hbm[i].at[l, :, pl.ds(hbase, hpc), :], bqkv.at[i]
        elif i == 3:
            src, dst = wo.at[l, pl.ds(hbase, hpc)], bo
        elif i < 6:
            src, dst = (wg, wu)[i - 4].at[l, :, pl.ds(fo, fw)], (bg, bu)[i - 4]
        else:
            src, dst = wd.at[l, pl.ds(fo, fw), :], bd
        return pltpu.make_async_copy(src, dst, wsem.at[i])

    for i in range(7):
        w_copy(0, i).start()

    for i in range(2):
        rows = slice(half * i, half * (i + 1))
        xs[pl.ds(my_rows[i], half), :] = x_in[rows, :]
        cos_t, sin_t = cos_in[rows, :], sin_in[rows, :]
        tab[0, pl.ds(my_rows[i], half), :] = jnp.concatenate([cos_t, cos_t], axis=-1)
        tab[1, pl.ds(my_rows[i], half), :] = jnp.concatenate([-sin_t, sin_t], axis=-1)
    gains[0] = ga[...].astype(F32)
    gains[1] = gm[...].astype(F32)

    barrier = pltpu.get_barrier_semaphore()
    for d in range(1, cp):
        pl.semaphore_signal(barrier, inc=1, device_id={"cp": lax.rem(me + d, cp)}, device_id_type=pl.DeviceIdType.MESH)
    pl.semaphore_wait(barrier, cp - 1)

    def first(rows, i):
        r = pl.ds(rows[i], half)
        return (rcopy(x_in.at[pl.ds(half * i, half), :], xs.at[r, :], isend.at[0, i], irecv.at[0, i], partner),
                rcopy(tab.at[:, r, :], tab.at[:, r, :], isend.at[1, i], irecv.at[1, i], partner))

    for i in range(2):
        for c in first(my_rows, i):
            c.start()
    for i in range(2):
        for c in first(pa_rows, i):
            c.wait_recv()
        for c in first(my_rows, i):
            c.wait_send()

    def norm(which, l):
        xv = xs[...].astype(F32)
        inv = lax.rsqrt(jnp.mean(xv * xv, axis=-1, keepdims=True) + NORM_EPS)
        hbuf[...] = (xv * inv * gains[which, pl.ds(l, 1), :]).astype(BF16)

    def partial_exchange(w, product, widths):
        starts = [sum(widths[:i]) for i in range(len(widths))]

        def pcopy(i):
            cols = pl.ds(starts[i], widths[i])
            return rcopy(pfull.at[:, cols], precv.at[w, :, cols], psend.at[w, i], precvs.at[w, i], partner)

        for i in range(len(widths)):
            cols = slice(starts[i], starts[i] + widths[i])
            pfull[:, cols] = product(cols)
            pcopy(i).start()
        for i in range(len(widths)):
            cols = slice(starts[i], starts[i] + widths[i])
            pcopy(i).wait()
            xs[:, cols] = (xs[:, cols].astype(F32) + (pfull[:, cols] + precv[w, :, cols])).astype(BF16)

    def layer(l, _):
        par = lax.rem(l, 2)

        def prefetch(i):
            @pl.when(l + 1 < n_layers)
            def _():
                w_copy(l + 1, i).start()

        norm(0, l)
        segs = (chip, nseg - 1 - chip)

        def send(t, r):
            for j in range(hpc):
                n = hbase + j
                rows = pl.ds(al(segs[r] * seg, seg), seg)

                @pl.when(n != me)
                def _():
                    rcopy(stage.at[t, j, pl.ds(seg * r, seg), :], nat.at[par, t, rows, :],
                          qsend.at[t, j, r], qrecv.at[par, t, segs[r]], n).start()

                @pl.when(n == me)
                def _():
                    nat[par, t, rows, :] = stage[t, j, seg * r:seg * (r + 1), :]

        for t in range(3):
            w_copy(l, t).wait()
            prod = dot(hbuf[...], bqkv[t].reshape(dim, hpc * hd))
            prefetch(t)
            for j in range(hpc):
                a = prod[:, hd * j:hd * (j + 1)]
                if t < 2:
                    a = a * tab[0] + pltpu.roll(a, hd // 2, 1) * tab[1]
                stage[t, j] = a.astype(BF16)
            send(t, 0)
        for t in range(3):
            send(t, 1)

        def wait_nat(t, r):
            for s in range(r * nseg // 2, (r + 1) * nseg // 2):
                src = worker(min(s, nseg - 1 - s))

                @pl.when(src != me)
                def _():
                    rcopy(stage.at[t, 0, pl.ds(0, seg), :], nat.at[par, t, pl.ds(s * seg, seg), :],
                          qsend.at[t, 0, 0], qrecv.at[par, t, s], src).wait_recv()

        def cache_copy(i):
            return pltpu.make_async_copy(nat.at[par, 2 * i], (kc, vc)[i].at[l], csem.at[i])

        qb = 256
        half_b = seq // qb // 2

        def softmax(b):
            n_keys = qb * (b + 1)
            q = nat[par, 1, pl.ds(qb * b, qb), :]
            k = nat[par, 0, pl.ds(0, n_keys), :]
            s = lax.dot_general(q, k, (((1,), (1,)), ((), ())), preferred_element_type=F32) * (hd ** -0.5)
            rows = lax.broadcasted_iota(jnp.int32, (qb, qb), 0)
            cols = lax.broadcasted_iota(jnp.int32, (qb, qb), 1)
            last = jnp.where(cols <= rows, s[:, n_keys - qb:], -jnp.inf)
            s = last if b == 0 else jnp.concatenate([s[:, :n_keys - qb], last], axis=1)
            e = jnp.exp(s - jnp.max(s, axis=-1, keepdims=True))
            return (e * (1.0 / jnp.sum(e, axis=-1, keepdims=True))).astype(BF16)

        def attend(b, p):
            onat[pl.ds(qb * b, qb), :] = dot(p, nat[par, 2, pl.ds(0, qb * (b + 1)), :]).astype(BF16)
            for s_i in range(b * qb // seg, (b + 1) * qb // seg):
                r = 1 if s_i >= nseg // 2 else 0
                dest = worker(min(s_i, nseg - 1 - s_i))
                cols_o = pl.ds(al(my_col * hd, hd), hd)

                @pl.when(dest != me)
                def _():
                    rcopy(onat.at[pl.ds(s_i * seg, seg), :], orecv.at[pl.ds(seg * r, seg), cols_o],
                          osend.at[s_i], orecvs.at[my_col, r], dest).start()

                @pl.when(dest == me)
                def _():
                    orecv[pl.ds(seg * r, seg), cols_o] = onat[s_i * seg:(s_i + 1) * seg, :]

        for t in range(3):
            wait_nat(t, 0)
        for b in range(half_b):
            attend(b, softmax(b))
        wait_nat(0, 1)
        cache_copy(0).start()
        wait_nat(1, 1)
        for b in range(half_b, 2 * half_b):
            probs[b - half_b, :, :qb * (b + 1)] = softmax(b)
        wait_nat(2, 1)
        cache_copy(1).start()
        for b in range(half_b, 2 * half_b):
            attend(b, probs[b - half_b, :, :qb * (b + 1)])

        for j in range(hpc):
            @pl.when(hbase + j != me)
            def _():
                for r in range(2):
                    rcopy(onat.at[pl.ds(0, seg), :], orecv.at[pl.ds(seg * r, seg), pl.ds(hd * j, hd)],
                          osend.at[0], orecvs.at[j, r], hbase + j).wait_recv()

        w_copy(l, 3).wait()
        partial_exchange(0, lambda cols: dot(orecv[...], bo[:, :, cols].reshape(hpc * hd, cols.stop - cols.start)),
                         (dim // 2, dim // 2))
        prefetch(3)
        norm(1, l)
        w_copy(l, 4).wait()
        w_copy(l, 5).wait()
        fc = fw // 2
        for i in range(2):
            cols = slice(fc * i, fc * (i + 1))
            a = (jax.nn.silu(dot(hbuf[...], bg[:, cols])) * dot(hbuf[...], bu[:, cols])).astype(BF16)
            if i == 0:
                cid = lax.broadcasted_iota(jnp.int32, (2 * seg, fc), 1)
                a = jnp.where(cid >= core * (fw - foff), a, jnp.zeros_like(a))
            act[:, cols] = a
        prefetch(4)
        prefetch(5)
        w_copy(l, 6).wait()
        partial_exchange(1, lambda cols: dot(act[...], bd[:, cols]), (dim // 2, dim // 4, dim // 4))
        prefetch(6)

        for i in range(2):
            cache_copy(i).wait()
        for t in range(3):
            for j in range(hpc):
                @pl.when(hbase + j != me)
                def _():
                    for r in range(2):
                        rcopy(stage.at[t, j, pl.ds(seg * r, seg), :], nat.at[par, t, pl.ds(0, seg), :],
                              qsend.at[t, j, r], qrecv.at[par, t, 0], hbase + j).wait_send()
        for s_i in range(nseg):
            dest = worker(min(s_i, nseg - 1 - s_i))

            @pl.when(dest != me)
            def _():
                rcopy(onat.at[pl.ds(s_i * seg, seg), :], orecv.at[pl.ds(0, seg), pl.ds(0, hd)],
                      osend.at[s_i], orecvs.at[0, 0], dest).wait_send()
        return 0

    lax.fori_loop(0, n_layers, layer, 0)
    for i in range(2):
        x_out[half * i:half * (i + 1), :] = xs[pl.ds(my_rows[i], half), :]


def copy_out(n, *refs):
    srcs, dsts, bufs, sem = refs[:n], refs[n:2 * n], refs[2 * n:3 * n], refs[3 * n]
    ins = [pltpu.make_async_copy(srcs[i], bufs[i], sem.at[0, i]) for i in range(n)]
    outs = [pltpu.make_async_copy(bufs[i], dsts[i], sem.at[1, i]) for i in range(n)]
    for c in ins:
        c.start()
    for i in range(n):
        ins[i].wait()
        outs[i].start()
    for c in outs:
        c.wait()


def solution(mesh):
    cp = mesh.shape["cp"]
    row_spec = P(("req", "cp"), None)
    rep = P()
    cache_spec = P(None, "req", "cp", None)

    def per_device(hidden, positions, ga, gm, wq, wk, wv, wo, wg, wu, wd):
        rows, dim = hidden.shape
        n_layers, _, heads, hd = wq.shape
        ff = wg.shape[2]
        seq = rows * cp
        half = rows // 2
        seg = rows
        nseg = seq // seg
        hpc = heads // 2
        tiles = ff // 128
        fw = -(-tiles // 4) * 2 * 128
        foff = ff - fw
        cfg = (cp, n_layers, half, seq, heads, hd, dim, fw, foff)
        cos_tab, sin_tab = rope_tables(positions, hd)
        vm = pl.BlockSpec(memory_space=pltpu.VMEM)
        hb = pl.BlockSpec(memory_space=pltpu.HBM)
        dma = pltpu.SemaphoreType.DMA
        V = pltpu.VMEM
        outs = (jax.ShapeDtypeStruct((rows, dim), BF16),
                jax.ShapeDtypeStruct((n_layers, seq, hd), BF16),
                jax.ShapeDtypeStruct((n_layers, seq, hd), BF16))
        res = pl.pallas_call(
            functools.partial(kernel, cfg),
            out_shape=outs,
            in_specs=[vm] * 5 + [hb] * 7,
            out_specs=(vm, hb, hb),
            scratch_shapes=[
                V((2 * seg, dim), BF16), V((2, n_layers, dim), F32), V((2, 2 * seg, hd), F32), V((2 * seg, dim), BF16),
                V((2 * seg, fw), BF16), V((3, hpc, 2 * seg, hd), BF16), V((2, 3, seq, hd), BF16), V((seq, hd), BF16),
                V((2, 256, seq), BF16), V((2 * seg, hpc * hd), BF16), V((2 * seg, dim), F32), V((2, 2 * seg, dim), F32),
                V((3, dim, hpc, hd), BF16), V((hpc, hd, dim), BF16), V((dim, fw), BF16), V((dim, fw), BF16), V((fw, dim), BF16),
                dma((7,)), dma((2,)), dma((2, 2)), dma((2, 2)), dma((2, 3)), dma((2, 3)),
                dma((3, hpc, 2)), dma((2, 3, nseg)), dma((nseg,)), dma((hpc, 2)),
            ],
            compiler_params=pltpu.CompilerParams(collective_id=0, has_side_effects=True, vmem_limit_bytes=67043328),
            name="prefill",
        )(hidden, cos_tab, sin_tab, ga, gm, wq, wk, wv, wo, wg, wu, wd)
        x, kc, vc = pl.pallas_call(
            functools.partial(copy_out, 3), out_shape=outs, in_specs=[hb] * 3, out_specs=(hb,) * 3,
            scratch_shapes=[V(o.shape, o.dtype) for o in outs] + [dma((2, 3))], name="copy_out",
        )(*res)
        return x, kc.reshape(n_layers, seq, 1, hd), vc.reshape(n_layers, seq, 1, hd)

    in_specs = (row_spec, P(("req", "cp"))) + (rep,) * 9
    return jax.shard_map(per_device, mesh=mesh, in_specs=in_specs, out_specs=(row_spec, cache_spec, cache_spec), check_vma=False)
```

time: 162 us -> 143 us (0.88)
  Pallas kernels: 150 us -> 141 us
  local copies, waits for them, and re-layouts: 8.49 us -> 0 us
    pallas_call x1 -> x2, Pallas kernels: 150 us -> 141 us  [the longest x1 138 us: per_device(): pl.pallas_call(functools.partial(kernel, cfg), out_shape=outs, in_specs=[...]
    unnamed x3 -> x0, local copies, waits for them, and re-layouts: 5.79 us -> none
    reshape x2 -> x0, local copies, waits for them, and re-layouts: 2.7 us -> none  [the longest x1 1.35 us: per_device(): ga.reshape(n_layers, 1, dim)]
where the time goes in v2:
time: 143 us
  Pallas kernels  141 us (99%)
  other arithmetic  1.5 us (1%)
    pallas_call x1, Pallas kernels, per_device(): pl.pallas_call(functools.partial(kernel, cfg), out_shape=outs, in_specs=[...  138 us

profile of v2, /device:TPU:23, one launch (start us, length us, event | category | flops | bytes accessed | tf_op | source)
XLA Modules:
  0.0 142.9 jit_solution(9907942117268235753)
XLA Ops:
  0.6 0.7 convert_element_type.3
  1.3 0.8 multiply_sine_fusion
  2.1 138.4 %prefill.1 = (bf16[64,2048]{1,0:T(8,128)(2,1)}, bf16[3,1024,128]{2,1,0:T(8,128)(2,1)}, bf16[3,1024,128]{2,1,0:T(8,128)(2,1)}) custom-call(bf16[64,2048]{1,0:T(8,128)(2,1)} %x_in.1, f32[64,64]{1,0:T(8,128)} %get-tuple-element.19.cos_in, f32[64,64]{1,0:T(8,128)} %get-tuple-element.18.sin_in, bf16[3,2048]{1,0:T(4,128)(2,1)} %ga.1, bf16[3,2048]{1,0:T(4,128)(2,1)} %gm.1, ...), custom_call_target="tpu_custom_call" | custom-call | tf_op jit(solution)/shard_map/prefill/pallas_call | solution.py:309
  140.5 2.4 %copy_out.1 = (bf16[64,2048]{1,0:T(8,128)(2,1)}, bf16[3,1024,128]{2,1,0:T(8,128)(2,1)}, bf16[3,1024,128]{2,1,0:T(8,128)(2,1)}) custom-call(bf16[64,2048]{1,0:T(8,128)(2,1)} %get-tuple-element.9.refs_0_, bf16[3,1024,128]{2,1,0:T(8,128)(2,1)} %get-tuple-element.10.refs_1_, bf16[3,1024,128]{2,1,0:T(8,128)(2,1)} %get-tuple-element.11.refs_2_), custom_call_target="tpu_custom_call" | custom-call | tf_op jit(solution)/shard_map/copy_out/pallas_call | solution.py:325
  (1 shorter events, 0.0 us)

commit v3 on v2

--- a/solution.py
+++ b/solution.py
@@ -99,79 +99,97 @@
         for c in first(my_rows, i):
             c.wait_send()
 
-    def norm(which, l):
-        xv = xs[...].astype(F32)
+    is_self = lax.rem(core + chip + chip // (nchip // 2), 2) == my_half
+
+    def wait_all(recv, sem):
+        def go(count):
+            ref = nat.at[0, 0, pl.ds(0, count * seg), :]
+            c = rcopy(ref, ref, sem, sem, partner)
+            if recv:
+                c.wait_recv()
+            else:
+                c.wait_send()
+
+        @pl.when(is_self)
+        def _():
+            go(nchip - 1)
+
+        @pl.when(jnp.logical_not(is_self))
+        def _():
+            go(nchip)
+
+    def half_rows(r):
+        return pl.ds(al(seg * r, seg), seg)
+
+    def norm(which, l, r):
+        rows = half_rows(r)
+        xv = xs[rows, :].astype(F32)
         inv = lax.rsqrt(jnp.mean(xv * xv, axis=-1, keepdims=True) + NORM_EPS)
-        hbuf[...] = (xv * inv * gains[which, pl.ds(l, 1), :]).astype(BF16)
-
-    def partial_exchange(w, product, widths):
+        hbuf[rows, :] = (xv * inv * gains[which, pl.ds(l, 1), :]).astype(BF16)
+
+    def chunks(widths):
         starts = [sum(widths[:i]) for i in range(len(widths))]
-
-        def pcopy(i):
-            cols = pl.ds(starts[i], widths[i])
-            return rcopy(pfull.at[:, cols], precv.at[w, :, cols], psend.at[w, i], precvs.at[w, i], partner)
-
-        for i in range(len(widths)):
-            cols = slice(starts[i], starts[i] + widths[i])
-            pfull[:, cols] = product(cols)
-            pcopy(i).start()
-        for i in range(len(widths)):
-            cols = slice(starts[i], starts[i] + widths[i])
-            pcopy(i).wait()
-            xs[:, cols] = (xs[:, cols].astype(F32) + (pfull[:, cols] + precv[w, :, cols])).astype(BF16)
-
-    def layer(l, _):
+        return [slice(c, c + w) for c, w in zip(starts, widths)]
+
+    def pcopy(w, r, i, cols):
+        rows, cs = half_rows(r), pl.ds(cols.start, cols.stop - cols.start)
+        return rcopy(pfull.at[rows, cs], precv.at[w, rows, cs], psend.at[w, r, i], precvs.at[w, r, i], partner)
+
+    def partial_start(w, r, product, widths):
+        for i, cols in enumerate(chunks(widths)):
+            pfull[half_rows(r), cols] = product(cols)
+            pcopy(w, r, i, cols).start()
+
+    def partial_finish(w, r, widths):
+        rows = half_rows(r)
+        for i, cols in enumerate(chunks(widths)):
+            pcopy(w, r, i, cols).wait()
+            xs[rows, cols] = (xs[rows, cols].astype(F32) + (pfull[rows, cols] + precv[w, rows, cols])).astype(BF16)
+
+    def w_wait(l, r, i):
+        @pl.when(r == 0)
+        def _():
+            w_copy(l, i).wait()
+
+    def prefetch(l, r, i):
+        @pl.when((r == 1) & (l + 1 < n_layers))
+        def _():
+            w_copy(l + 1, i).start()
+
+    wo_widths = (dim // 2, dim // 2)
+    wd_widths = (dim // 2, dim // 4, dim // 4)
+    qb = 256
+    half_b = seq // qb // 2
+
+    def qkv(l, r):
         par = lax.rem(l, 2)
-
-        def prefetch(i):
-            @pl.when(l + 1 < n_layers)
-            def _():
-                w_copy(l + 1, i).start()
-
-        norm(0, l)
-        segs = (chip, nseg - 1 - chip)
-
-        def send(t, r):
-            for j in range(hpc):
-                n = hbase + j
-                rows = pl.ds(al(segs[r] * seg, seg), seg)
-
-                @pl.when(n != me)
-                def _():
-                    rcopy(stage.at[t, j, pl.ds(seg * r, seg), :], nat.at[par, t, rows, :],
-                          qsend.at[t, j, r], qrecv.at[par, t, segs[r]], n).start()
-
-                @pl.when(n == me)
-                def _():
-                    nat[par, t, rows, :] = stage[t, j, seg * r:seg * (r + 1), :]
-
+        hrows = half_rows(r)
+        norm(0, l, r)
+        seg_id = chip + r * (nseg - 1 - 2 * chip)
         for t in range(3):
-            w_copy(l, t).wait()
-            prod = dot(hbuf[...], bqkv[t].reshape(dim, hpc * hd))
-            prefetch(t)
+            w_wait(l, r, t)
+            prod = dot(hbuf[hrows, :], bqkv[t].reshape(dim, hpc * hd))
+            prefetch(l, r, t)
             for j in range(hpc):
                 a = prod[:, hd * j:hd * (j + 1)]
                 if t < 2:
-                    a = a * tab[0] + pltpu.roll(a, hd // 2, 1) * tab[1]
-                stage[t, j] = a.astype(BF16)
-            send(t, 0)
-        for t in range(3):
-            send(t, 1)
-
-        def wait_nat(t, r):
-            for s in range(r * nseg // 2, (r + 1) * nseg // 2):
-                src = worker(min(s, nseg - 1 - s))
-
-                @pl.when(src != me)
+                    a = a * tab[0, hrows, :] + pltpu.roll(a, hd // 2, 1) * tab[1, hrows, :]
+                stage[t, j, hrows, :] = a.astype(BF16)
+            rows = pl.ds(al(seg_id * seg, seg), seg)
+            for j in range(hpc):
+                n = hbase + j
+
+                @pl.when(n != me)
                 def _():
-                    rcopy(stage.at[t, 0, pl.ds(0, seg), :], nat.at[par, t, pl.ds(s * seg, seg), :],
-                          qsend.at[t, 0, 0], qrecv.at[par, t, s], src).wait_recv()
-
-        def cache_copy(i):
-            return pltpu.make_async_copy(nat.at[par, 2 * i], (kc, vc)[i].at[l], csem.at[i])
-
-        qb = 256
-        half_b = seq // qb // 2
+                    rcopy(stage.at[t, j, hrows, :], nat.at[par, t, rows, :],
+                          qsend.at[t, r], qrecv.at[par, t, r], n).start()
+
+                @pl.when(n == me)
+                def _():
+                    nat[par, t, rows, :] = stage[t, j, hrows, :]
+
+    def attention(l, r):
+        par = lax.rem(l, 2)
 
         def softmax(b):
             n_keys = qb * (b + 1)
@@ -188,80 +206,92 @@
         def attend(b, p):
             onat[pl.ds(qb * b, qb), :] = dot(p, nat[par, 2, pl.ds(0, qb * (b + 1)), :]).astype(BF16)
             for s_i in range(b * qb // seg, (b + 1) * qb // seg):
-                r = 1 if s_i >= nseg // 2 else 0
                 dest = worker(min(s_i, nseg - 1 - s_i))
                 cols_o = pl.ds(al(my_col * hd, hd), hd)
 
                 @pl.when(dest != me)
                 def _():
                     rcopy(onat.at[pl.ds(s_i * seg, seg), :], orecv.at[pl.ds(seg * r, seg), cols_o],
-                          osend.at[s_i], orecvs.at[my_col, r], dest).start()
+                          osend.at[r], orecvs.at[r], dest).start()
 
                 @pl.when(dest == me)
                 def _():
                     orecv[pl.ds(seg * r, seg), cols_o] = onat[s_i * seg:(s_i + 1) * seg, :]
 
+        if r == 0:
+            for t in range(3):
+                wait_all(True, qrecv.at[par, t, 0])
+            for b in range(half_b):
+                attend(b, softmax(b))
+        else:
+            wait_all(True, qrecv.at[par, 0, 1])
+            cache_copy(l, 0).start()
+            wait_all(True, qrecv.at[par, 1, 1])
+            for b in range(half_b, 2 * half_b):
+                probs[b - half_b, :, :qb * (b + 1)] = softmax(b)
+            wait_all(True, qrecv.at[par, 2, 1])
+            cache_copy(l, 1).start()
+            for b in range(half_b, 2 * half_b):
+                attend(b, probs[b - half_b, :, :qb * (b + 1)])
+
+    def cache_copy(l, i):
+        return pltpu.make_async_copy(nat.at[lax.rem(l, 2), 2 * i], (kc, vc)[i].at[l], csem.at[i])
+
+    def post(l, r):
+        hrows = half_rows(r)
+        wait_all(True, orecvs.at[r])
+        w_wait(l, r, 3)
+        partial_start(0, r, lambda cols: dot(orecv[hrows, :], bo[:, :, cols].reshape(hpc * hd, cols.stop - cols.start)), wo_widths)
+        prefetch(l, r, 3)
         for t in range(3):
-            wait_nat(t, 0)
-        for b in range(half_b):
-            attend(b, softmax(b))
-        wait_nat(0, 1)
-        cache_copy(0).start()
-        wait_nat(1, 1)
-        for b in range(half_b, 2 * half_b):
-            probs[b - half_b, :, :qb * (b + 1)] = softmax(b)
-        wait_nat(2, 1)
-        cache_copy(1).start()
-        for b in range(half_b, 2 * half_b):
-            attend(b, probs[b - half_b, :, :qb * (b + 1)])
-
-        for j in range(hpc):
-            @pl.when(hbase + j != me)
-            def _():
-                for r in range(2):
-                    rcopy(onat.at[pl.ds(0, seg), :], orecv.at[pl.ds(seg * r, seg), pl.ds(hd * j, hd)],
-                          osend.at[0], orecvs.at[j, r], hbase + j).wait_recv()
-
-        w_copy(l, 3).wait()
-        partial_exchange(0, lambda cols: dot(orecv[...], bo[:, :, cols].reshape(hpc * hd, cols.stop - cols.start)),
-                         (dim // 2, dim // 2))
-        prefetch(3)
-        norm(1, l)
-        w_copy(l, 4).wait()
-        w_copy(l, 5).wait()
+            wait_all(False, qsend.at[t, r])
+        wait_all(False, osend.at[r])
+        partial_finish(0, r, wo_widths)
+        norm(1, l, r)
+        w_wait(l, r, 4)
+        w_wait(l, r, 5)
         fc = fw // 2
         for i in range(2):
             cols = slice(fc * i, fc * (i + 1))
-            a = (jax.nn.silu(dot(hbuf[...], bg[:, cols])) * dot(hbuf[...], bu[:, cols])).astype(BF16)
+            a = (jax.nn.silu(dot(hbuf[hrows, :], bg[:, cols])) * dot(hbuf[hrows, :], bu[:, cols])).astype(BF16)
             if i == 0:
-                cid = lax.broadcasted_iota(jnp.int32, (2 * seg, fc), 1)
+                cid = lax.broadcasted_iota(jnp.int32, (seg, fc), 1)
                 a = jnp.where(cid >= core * (fw - foff), a, jnp.zeros_like(a))
-            act[:, cols] = a
-        prefetch(4)
-        prefetch(5)
-        w_copy(l, 6).wait()
-        partial_exchange(1, lambda cols: dot(act[...], bd[:, cols]), (dim // 2, dim // 4, dim // 4))
-        prefetch(6)
-
-        for i in range(2):
-            cache_copy(i).wait()
-        for t in range(3):
-            for j in range(hpc):
-                @pl.when(hbase + j != me)
-                def _():
-                    for r in range(2):
-                        rcopy(stage.at[t, j, pl.ds(seg * r, seg), :], nat.at[par, t, pl.ds(0, seg), :],
-                              qsend.at[t, j, r], qrecv.at[par, t, 0], hbase + j).wait_send()
-        for s_i in range(nseg):
-            dest = worker(min(s_i, nseg - 1 - s_i))
-
-            @pl.when(dest != me)
+            act[hrows, cols] = a
+        prefetch(l, r, 4)
+        prefetch(l, r, 5)
+        w_wait(l, r, 6)
+        partial_start(1, r, lambda cols: dot(act[hrows, :], bd[:, cols]), wd_widths)
+        prefetch(l, r, 6)
+
+    def step(i, _):
+        l_now, r_now = (i + 1) // 2 - 1, lax.rem(i + 1, 2)
+        r_next = lax.rem(i, 2)
+        for r in range(2):
+            @pl.when((i > 0) & (r_now == r))
             def _():
-                rcopy(onat.at[pl.ds(s_i * seg, seg), :], orecv.at[pl.ds(0, seg), pl.ds(0, hd)],
-                      osend.at[s_i], orecvs.at[0, 0], dest).wait_send()
+                attention(l_now, r)
+
+        @pl.when(i > 1)
+        def _():
+            partial_finish(1, r_next, wd_widths)
+
+        @pl.when(i < 2 * n_layers)
+        def _():
+            qkv(i // 2, r_next)
+
+        @pl.when(i > 0)
+        def _():
+            post(l_now, r_now)
+
+        @pl.when((i > 0) & (r_now == 1))
+        def _():
+            for c in range(2):
+                cache_copy(l_now, c).wait()
         return 0
 
-    lax.fori_loop(0, n_layers, layer, 0)
+    lax.fori_loop(0, 2 * n_layers + 1, step, 0)
+    partial_finish(1, 1, wd_widths)
     for i in range(2):
         x_out[half * i:half * (i + 1), :] = xs[pl.ds(my_rows[i], half), :]
 
@@ -316,8 +346,8 @@
                 V((2 * seg, fw), BF16), V((3, hpc, 2 * seg, hd), BF16), V((2, 3, seq, hd), BF16), V((seq, hd), BF16),
                 V((2, 256, seq), BF16), V((2 * seg, hpc * hd), BF16), V((2 * seg, dim), F32), V((2, 2 * seg, dim), F32),
                 V((3, dim, hpc, hd), BF16), V((hpc, hd, dim), BF16), V((dim, fw), BF16), V((dim, fw), BF16), V((fw, dim), BF16),
-                dma((7,)), dma((2,)), dma((2, 2)), dma((2, 2)), dma((2, 3)), dma((2, 3)),
-                dma((3, hpc, 2)), dma((2, 3, nseg)), dma((nseg,)), dma((hpc, 2)),
+                dma((7,)), dma((2,)), dma((2, 2)), dma((2, 2)), dma((2, 2, 3)), dma((2, 2, 3)),
+                dma((3, 2)), dma((2, 3, 2)), dma((2,)), dma((2,)),
             ],
             compiler_params=pltpu.CompilerParams(collective_id=0, has_side_effects=True, vmem_limit_bytes=67043328),
             name="prefill",

time: 143 us -> 137 us (0.958)
  Pallas kernels: 141 us -> 134 us
    pallas_call x1, Pallas kernels: 138 us -> 132 us  [per_device(): pl.pallas_call(functools.partial(kernel, cfg), out_shape=outs, in_specs=[...]
where the time goes in v3:
time: 137 us
  Pallas kernels  134 us (98%)
  other arithmetic  1.5 us (1%)
    pallas_call x1, Pallas kernels, per_device(): pl.pallas_call(functools.partial(kernel, cfg), out_shape=outs, in_specs=[...  132 us

profile of v3, /device:TPU:23, one launch (start us, length us, event | category | flops | bytes accessed | tf_op | source)
XLA Modules:
  0.0 136.6 jit_solution(7636691596924639668)
XLA Ops:
  0.6 0.7 convert_element_type.3
  1.3 0.8 multiply_sine_fusion
  2.1 132.0 %prefill.1 = (bf16[64,2048]{1,0:T(8,128)(2,1)}, bf16[3,1024,128]{2,1,0:T(8,128)(2,1)}, bf16[3,1024,128]{2,1,0:T(8,128)(2,1)}) custom-call(bf16[64,2048]{1,0:T(8,128)(2,1)} %x_in.1, f32[64,64]{1,0:T(8,128)} %get-tuple-element.19.cos_in, f32[64,64]{1,0:T(8,128)} %get-tuple-element.18.sin_in, bf16[3,2048]{1,0:T(4,128)(2,1)} %ga.1, bf16[3,2048]{1,0:T(4,128)(2,1)} %gm.1, ...), custom_call_target="tpu_custom_call" | custom-call | tf_op jit(solution)/shard_map/prefill/pallas_call | solution.py:339
  134.1 2.4 %copy_out.1 = (bf16[64,2048]{1,0:T(8,128)(2,1)}, bf16[3,1024,128]{2,1,0:T(8,128)(2,1)}, bf16[3,1024,128]{2,1,0:T(8,128)(2,1)}) custom-call(bf16[64,2048]{1,0:T(8,128)(2,1)} %get-tuple-element.9.refs_0_, bf16[3,1024,128]{2,1,0:T(8,128)(2,1)} %get-tuple-element.10.refs_1_, bf16[3,1024,128]{2,1,0:T(8,128)(2,1)} %get-tuple-element.11.refs_2_), custom_call_target="tpu_custom_call" | custom-call | tf_op jit(solution)/shard_map/copy_out/pallas_call | solution.py:355
  (1 shorter events, 0.0 us)

commit v4 on v3

--- a/solution.py
+++ b/solution.py
@@ -79,6 +79,7 @@
         tab[1, pl.ds(my_rows[i], half), :] = jnp.concatenate([-sin_t, sin_t], axis=-1)
     gains[0] = ga[...].astype(F32)
     gains[1] = gm[...].astype(F32)
+    hbuf[...] = jnp.zeros_like(hbuf)
 
     barrier = pltpu.get_barrier_semaphore()
     for d in range(1, cp):
@@ -135,9 +136,9 @@
         rows, cs = half_rows(r), pl.ds(cols.start, cols.stop - cols.start)
         return rcopy(pfull.at[rows, cs], precv.at[w, rows, cs], psend.at[w, r, i], precvs.at[w, r, i], partner)
 
-    def partial_start(w, r, product, widths):
+    def partial_start(w, r, rows, product, widths):
         for i, cols in enumerate(chunks(widths)):
-            pfull[half_rows(r), cols] = product(cols)
+            pfull[rows, cols] = product(cols)
             pcopy(w, r, i, cols).start()
 
     def partial_finish(w, r, widths):
@@ -176,17 +177,21 @@
                     a = a * tab[0, hrows, :] + pltpu.roll(a, hd // 2, 1) * tab[1, hrows, :]
                 stage[t, j, hrows, :] = a.astype(BF16)
             rows = pl.ds(al(seg_id * seg, seg), seg)
-            for j in range(hpc):
-                n = hbase + j
-
-                @pl.when(n != me)
-                def _():
+            for d in range(hpc):
+                j = lax.rem(my_col + 1 + d, hpc)
+
+                def go():
                     rcopy(stage.at[t, j, hrows, :], nat.at[par, t, rows, :],
-                          qsend.at[t, r], qrecv.at[par, t, r], n).start()
-
-                @pl.when(n == me)
-                def _():
-                    nat[par, t, rows, :] = stage[t, j, hrows, :]
+                          qsend.at[t, r], qrecv.at[par, t, r], hbase + j).start()
+
+                if d < hpc - 1:
+                    go()
+                else:
+                    pl.when(jnp.logical_not(is_self))(go)
+
+                    @pl.when(is_self)
+                    def _():
+                        nat[par, t, rows, :] = stage[t, j, hrows, :]
 
     def attention(l, r):
         par = lax.rem(l, 2)
@@ -241,7 +246,7 @@
         hrows = half_rows(r)
         wait_all(True, orecvs.at[r])
         w_wait(l, r, 3)
-        partial_start(0, r, lambda cols: dot(orecv[hrows, :], bo[:, :, cols].reshape(hpc * hd, cols.stop - cols.start)), wo_widths)
+        partial_start(0, r, hrows, lambda cols: dot(orecv[hrows, :], bo[:, :, cols].reshape(hpc * hd, cols.stop - cols.start)), wo_widths)
         prefetch(l, r, 3)
         for t in range(3):
             wait_all(False, qsend.at[t, r])
@@ -253,15 +258,15 @@
         fc = fw // 2
         for i in range(2):
             cols = slice(fc * i, fc * (i + 1))
-            a = (jax.nn.silu(dot(hbuf[hrows, :], bg[:, cols])) * dot(hbuf[hrows, :], bu[:, cols])).astype(BF16)
+            a = (jax.nn.silu(dot(hbuf[...], bg[:, cols])) * dot(hbuf[...], bu[:, cols])).astype(BF16)
             if i == 0:
-                cid = lax.broadcasted_iota(jnp.int32, (seg, fc), 1)
+                cid = lax.broadcasted_iota(jnp.int32, (2 * seg, fc), 1)
                 a = jnp.where(cid >= core * (fw - foff), a, jnp.zeros_like(a))
-            act[hrows, cols] = a
+            act[:, cols] = a
         prefetch(l, r, 4)
         prefetch(l, r, 5)
         w_wait(l, r, 6)
-        partial_start(1, r, lambda cols: dot(act[hrows, :], bd[:, cols]), wd_widths)
+        partial_start(1, r, slice(None), lambda cols: dot(act[...], bd[:, cols]), wd_widths)
         prefetch(l, r, 6)
 
     def step(i, _):

time: 137 us -> 130 us (0.949)
  Pallas kernels: 134 us -> 127 us
    pallas_call x1, Pallas kernels: 132 us -> 125 us  [per_device(): pl.pallas_call(functools.partial(kernel, cfg), out_shape=outs, in_specs=[...]
where the time goes in v4:
time: 130 us; the launch traced here: 129 us
  Pallas kernels  127 us (98%)
  other arithmetic  1.5 us (1%)
    pallas_call x1, Pallas kernels, per_device(): pl.pallas_call(functools.partial(kernel, cfg), out_shape=outs, in_specs=[...  125 us

profile of v4, /device:TPU:23, one launch (start us, length us, event | category | flops | bytes accessed | tf_op | source)
XLA Modules:
  0.0 129.2 jit_solution(4241024441951240020)
XLA Ops:
  0.6 0.7 convert_element_type.3
  1.3 0.8 multiply_sine_fusion
  2.1 124.7 %prefill.1 = (bf16[64,2048]{1,0:T(8,128)(2,1)}, bf16[3,1024,128]{2,1,0:T(8,128)(2,1)}, bf16[3,1024,128]{2,1,0:T(8,128)(2,1)}) custom-call(bf16[64,2048]{1,0:T(8,128)(2,1)} %x_in.1, f32[64,64]{1,0:T(8,128)} %get-tuple-element.19.cos_in, f32[64,64]{1,0:T(8,128)} %get-tuple-element.18.sin_in, bf16[3,2048]{1,0:T(4,128)(2,1)} %ga.1, bf16[3,2048]{1,0:T(4,128)(2,1)} %gm.1, ...), custom_call_target="tpu_custom_call" | custom-call | tf_op jit(solution)/shard_map/prefill/pallas_call | solution.py:344
  126.8 2.4 %copy_out.1 = (bf16[64,2048]{1,0:T(8,128)(2,1)}, bf16[3,1024,128]{2,1,0:T(8,128)(2,1)}, bf16[3,1024,128]{2,1,0:T(8,128)(2,1)}) custom-call(bf16[64,2048]{1,0:T(8,128)(2,1)} %get-tuple-element.9.refs_0_, bf16[3,1024,128]{2,1,0:T(8,128)(2,1)} %get-tuple-element.10.refs_1_, bf16[3,1024,128]{2,1,0:T(8,128)(2,1)} %get-tuple-element.11.refs_2_), custom_call_target="tpu_custom_call" | custom-call | tf_op jit(solution)/shard_map/copy_out/pallas_call | solution.py:360
  (1 shorter events, 0.0 us)
